TPU v7x, 32 devices: a whole 2x2x4 slice. The times are simulated.
32 devices in a mesh: section: 2 (over y), mp: 16 (over z, x, core).
Axes of the slice: x: 2, y: 2, z: 4, core: 2. Of those that a mesh axis runs over, the one named last changes fastest.
Arguments:
- features: bfloat16 [4, 32, 8192], P(None, None, 'mp'), may hold values from -6 to 6
- labels: int32 [4, 32], replicated, may hold values 0 or 1
- weights: bfloat16 [2, 8192, 8192], P('section', None, 'mp'), may hold values from -1.78986404 to 1.78986404
- vectors: float32 [2, 8192], P('section', 'mp'), may hold values from -6 to 6
- head_weight: float32 [8192], P('mp'), may hold values from -0.0625 to 0.0625
Outputs:
- weight_grad: bfloat16 [2, 8192, 8192], P('section', None, 'mp')
- new_vectors: float32 [2, 8192], P('section', 'mp')
- rank_coef: float32 [2], P('section')
All inputs are finite; a program needn't handle non-finite values.
Results may differ from a plain program's by a relative error of at most 0.015.
Values may be sent and summed in bfloat16 or wider, within the bound.
No kernel may reach another device: no remote copies, remote signals or barrier semaphores. Data moves between devices by JAX's collectives and lax.ppermute only.
A program may use at most 64 MiB of HBM per device.

v0:
```python
import jax
import jax.numpy as jnp
from jax import lax
from jax.sharding import PartitionSpec as P

loss_scale = 32.0
tiny_eps = 1e-06


def shifted(block, axis, distance):
    devices = range(lax.axis_size(axis))
    route = [(i - distance, i) for i in devices if i - distance in devices]
    return lax.ppermute(block, axis, route)


def silu_slope(pre_act):
    gate_val = jax.nn.sigmoid(pre_act)
    return gate_val * (1.0 + pre_act * (1.0 - gate_val))


def keep_slot(stored, update, micro_slot, is_live):
    previous = lax.dynamic_index_in_dim(stored, micro_slot, 0, keepdims=False)
    return lax.dynamic_update_index_in_dim(
        stored, jnp.where(is_live, update, previous), micro_slot, 0
    )


def power_step(weight, vector_u):
    vector_bf = vector_u.astype(jnp.bfloat16)
    left_sum = lax.psum(jnp.dot(weight, vector_bf, preferred_element_type=jnp.float32), "mp")
    vector_v = (left_sum * lax.rsqrt(jnp.sum(left_sum * left_sum) + tiny_eps)).astype(jnp.bfloat16)
    right_part = jnp.dot(vector_v, weight, preferred_element_type=jnp.float32)
    norm_total = lax.psum(jnp.sum(right_part * right_part), "mp")
    spectral = jnp.sqrt(norm_total + tiny_eps)
    return (spectral, right_part / spectral)


def on_device(features, labels, weights, vectors, head_weight):
    weight = weights[0]
    vector_u = vectors[0]
    micro_count, batch_rows, local_cols = features.shape
    full_width = weight.shape[0]
    sections = lax.axis_size("section")
    section_index = lax.axis_index("section")
    tick_count = micro_count + sections - 1
    sign_all = (2 * labels - 1).astype(jnp.float32)
    spectral_init, new_init = power_step(weight, vector_u)

    def forward_tick(tick_now, state_all):
        incoming, inputs_all, pre_all, logits_all, spectral, new_u = state_all
        micro_index = tick_now - section_index
        is_live = (micro_index >= 0) & (micro_index < micro_count)
        micro_slot = jnp.clip(micro_index, 0, micro_count - 1)
        first_input = lax.dynamic_index_in_dim(features, micro_slot, 0, keepdims=False)
        layer_in = jnp.where(section_index == 0, first_input, incoming)
        shard_piece = lax.all_gather(layer_in, "mp", axis=1, tiled=True)
        accum_part = jnp.dot(shard_piece, weight, preferred_element_type=jnp.float32)
        whole_rows = shard_piece
        accum_part, whole_rows = (accum_part, whole_rows)
        pre_act = accum_part / spectral
        layer_out = (layer_in.astype(jnp.float32) + jax.nn.silu(pre_act)).astype(jnp.bfloat16)
        partial_logit = jnp.sum(layer_out.astype(jnp.float32) * head_weight[None, :], axis=1)
        inputs_all = keep_slot(inputs_all, whole_rows, micro_slot, is_live)
        pre_all = keep_slot(pre_all, pre_act, micro_slot, is_live)
        logits_all = keep_slot(
            logits_all, partial_logit, micro_slot, is_live & (section_index == sections - 1)
        )
        incoming = shifted(layer_out, "section", 1)
        return (incoming, inputs_all, pre_all, logits_all, spectral, new_u)

    start_state = (
        jnp.zeros((batch_rows, local_cols), jnp.bfloat16),
        jnp.zeros((micro_count, batch_rows, full_width), jnp.bfloat16),
        jnp.zeros((micro_count, batch_rows, local_cols), jnp.float32),
        jnp.zeros((micro_count, batch_rows), jnp.float32),
        spectral_init,
        new_init,
    )
    _, inputs_all, pre_all, partial_logits, spectral, new_u = lax.fori_loop(
        0, tick_count, forward_tick, start_state
    )
    logits_all = lax.psum(partial_logits, "mp")

    def backward_tick(tick_now, state_all):
        incoming, grad_all = state_all
        micro_index = tick_now - (sections - 1 - section_index)
        is_live = (micro_index >= 0) & (micro_index < micro_count)
        micro_slot = jnp.clip(micro_index, 0, micro_count - 1)
        sign_row = lax.dynamic_index_in_dim(sign_all, micro_slot, 0, keepdims=False)
        logit_row = lax.dynamic_index_in_dim(logits_all, micro_slot, 0, keepdims=False)
        top_scale = -loss_scale * sign_row * jax.nn.sigmoid(-sign_row * logit_row)
        top_grad = (top_scale[:, None] * head_weight[None, :]).astype(jnp.bfloat16)
        grad_out = jnp.where(section_index == sections - 1, top_grad, incoming)
        pre_act = lax.dynamic_index_in_dim(pre_all, micro_slot, 0, keepdims=False)
        grad_pre = (grad_out.astype(jnp.float32) * silu_slope(pre_act)).astype(jnp.bfloat16)
        partial_term = lax.dot_general(
            grad_pre, weight, (((1,), (1,)), ((), ())), preferred_element_type=jnp.float32
        )
        received = lax.all_to_all(
            partial_term.astype(jnp.bfloat16), "mp", split_axis=1, concat_axis=0, tiled=True
        ).astype(partial_term.dtype)
        back_sum = jnp.sum(received.reshape(-1, batch_rows, local_cols), axis=0)
        grad_in = (grad_out.astype(jnp.float32) + back_sum / spectral).astype(jnp.bfloat16)
        grad_all = keep_slot(grad_all, grad_pre, micro_slot, is_live)
        incoming = shifted(grad_in, "section", -1)
        return (incoming, grad_all)

    back_state = (
        jnp.zeros((batch_rows, local_cols), jnp.bfloat16),
        jnp.zeros((micro_count, batch_rows, local_cols), jnp.bfloat16),
    )
    _, grad_all = lax.fori_loop(0, tick_count, backward_tick, back_state)
    whole_rows = inputs_all.reshape(micro_count * batch_rows, full_width)
    grad_rows = grad_all.reshape(micro_count * batch_rows, local_cols)
    outer_sum = lax.dot_general(
        whole_rows, grad_rows, (((0,), (0,)), ((), ())), preferred_element_type=jnp.float32
    )
    weight_grad = (outer_sum / spectral).astype(jnp.bfloat16)
    inner_total = lax.psum(jnp.sum(outer_sum * weight.astype(jnp.float32)), "mp")
    rank_coef = inner_total / (spectral * spectral)
    return (weight_grad[None], new_u[None], rank_coef.reshape(1))


def solution(mesh):
    placed = (P(None, None, "mp"), P(), P("section", None, "mp"), P("section", "mp"), P("mp"))
    return jax.shard_map(
        on_device,
        mesh=mesh,
        in_specs=placed,
        out_specs=(P("section", None, "mp"), P("section", "mp"), P("section")),
        check_vma=False,
    )
```

profile of v0, /device:TPU:0, one launch (start us, length us, event | category | flops | bytes accessed | tf_op | source)
XLA Modules:
  0.0 495.4 jit_solution(9324954132209440340)
XLA Ops:
  0.6 5.6 %fusion.15 = f32[1,8192]{1,0:T(1,128)S(1)} fusion(f32[1,512]{1,0:T(1,128)} %param.12, bf16[1,8192,512]{2,1,0:T(8,128)(2,1)} %param.11), kind=kOutput, calls=%fused_computation.44 | convolution fusion | flops 8389120 | bytes 8423424 | tf_op jit(solution)/shard_map/dot_general | solution.py:30
  6.3 63.0 %psum.28 = f32[8192]{0:T(1024)S(1)} all-reduce(f32[8192]{0:T(1024)S(1)} %bitcast.113), channel_id=1, replica_groups=mesh['section'=2,'mp'=16] {'mp'}, use_global_device_ids=true, to_apply=%region_0.0 | all-reduce | flops 8192 | bytes 65536 | tf_op jit(solution)/shard_map/psum | solution.py:30
  70.6 4.6 fusion.18
  75.8 30.1 %psum.29 = f32[]{:T(128)} all-reduce(f32[]{:T(128)} %multiply_reduce_fusion.2), channel_id=1, replica_groups=mesh['section'=2,'mp'=16] {'mp'}, use_global_device_ids=true, to_apply=%region_3.0 | all-reduce | flops 1 | bytes 8 | tf_op jit(solution)/shard_map/psum | solution.py:33
  107.4 158.8 %while.37 = (s32[]{:T(128)}, bf16[32,512]{1,0:T(8,128)(2,1)}, bf16[4,32,8192]{2,1,0:T(8,128)(2,1)S(1)}, f32[4,32,512]{2,1,0:T(8,128)S(1)}, f32[4,32]{1,0:T(4,128...) while((s32[]{:T(128)}, bf16[32,512]{1,0:T(8,128)(2,1)}, ...), condition=%wide.region_6.7_spmd, body=%wide.region_4.6_spmd.sunk | while | flops 268910592 | bytes 12782621 | solution.py:79
  108.2 18.7 %all_gather.9 = bf16[32,8192]{1,0:T(8,128)(2,1)S(1)} all-gather(bf16[32,512]{1,0:T(8,128)(2,1)S(1)} %bitcast_select_fusion.5), channel_id=1, replica_groups=mesh['section'=2,'mp'=16] {'mp'}, dimensions={1}, use_global_device_ids=true | all-gather | bytes 557056 | tf_op jit(solution)/shard_map/while/body/eval_jaxpr/all_gather | solution.py:56
  126.9 5.7 %multiply_reduce_fusion.4 = (f32[32]{0:T(128)S(1)}, bf16[32,512]{1,0:T(8,128)(2,1)}, f32[32,512]{1,0:T(8,128)S(1)}) fusion(f32[512]{0:T(512)S(1)} %get-tuple-element.704, bf16[32,512]{1,0:T(8,128)(2,1)S(1)} %bitcast_select_fusion.5, f32[]{:T(128)} %get-tuple-element.702, bf16[32,8192]{1,0:T(8,128)(2,1)S(1)} %all_gather.9, ...), kind=kOutput, calls=%fused_computation.5.clone.1 | convolution fusion | flops 268615648 | bytes 9046148 | tf_op jit(solution)/shard_map/while/body/eval_jaxpr/dot_general | solution.py:57
  132.5 4.0 collective-permute-start
  138.6 20.4 %all_gather.9 = bf16[32,8192]{1,0:T(8,128)(2,1)S(1)} all-gather(bf16[32,512]{1,0:T(8,128)(2,1)S(1)} %bitcast_select_fusion.5), channel_id=1, replica_groups=mesh['section'=2,'mp'=16] {'mp'}, dimensions={1}, use_global_device_ids=true | all-gather | bytes 557056 | tf_op jit(solution)/shard_map/while/body/eval_jaxpr/all_gather | solution.py:56
  159.1 5.7 %multiply_reduce_fusion.4 = (f32[32]{0:T(128)S(1)}, bf16[32,512]{1,0:T(8,128)(2,1)}, f32[32,512]{1,0:T(8,128)S(1)}) fusion(f32[512]{0:T(512)S(1)} %get-tuple-element.704, bf16[32,512]{1,0:T(8,128)(2,1)S(1)} %bitcast_select_fusion.5, f32[]{:T(128)} %get-tuple-element.702, bf16[32,8192]{1,0:T(8,128)(2,1)S(1)} %all_gather.9, ...), kind=kOutput, calls=%fused_computation.5.clone.1 | convolution fusion | flops 268615648 | bytes 9046148 | tf_op jit(solution)/shard_map/while/body/eval_jaxpr/dot_general | solution.py:57
  164.7 4.8 collective-permute-start
  171.6 18.7 %all_gather.9 = bf16[32,8192]{1,0:T(8,128)(2,1)S(1)} all-gather(bf16[32,512]{1,0:T(8,128)(2,1)S(1)} %bitcast_select_fusion.5), channel_id=1, replica_groups=mesh['section'=2,'mp'=16] {'mp'}, dimensions={1}, use_global_device_ids=true | all-gather | bytes 557056 | tf_op jit(solution)/shard_map/while/body/eval_jaxpr/all_gather | solution.py:56
  190.3 5.7 %multiply_reduce_fusion.4 = (f32[32]{0:T(128)S(1)}, bf16[32,512]{1,0:T(8,128)(2,1)}, f32[32,512]{1,0:T(8,128)S(1)}) fusion(f32[512]{0:T(512)S(1)} %get-tuple-element.704, bf16[32,512]{1,0:T(8,128)(2,1)S(1)} %bitcast_select_fusion.5, f32[]{:T(128)} %get-tuple-element.702, bf16[32,8192]{1,0:T(8,128)(2,1)S(1)} %all_gather.9, ...), kind=kOutput, calls=%fused_computation.5.clone.1 | convolution fusion | flops 268615648 | bytes 9046148 | tf_op jit(solution)/shard_map/while/body/eval_jaxpr/dot_general | solution.py:57
  195.9 4.8 collective-permute-start
  202.8 20.4 %all_gather.9 = bf16[32,8192]{1,0:T(8,128)(2,1)S(1)} all-gather(bf16[32,512]{1,0:T(8,128)(2,1)S(1)} %bitcast_select_fusion.5), channel_id=1, replica_groups=mesh['section'=2,'mp'=16] {'mp'}, dimensions={1}, use_global_device_ids=true | all-gather | bytes 557056 | tf_op jit(solution)/shard_map/while/body/eval_jaxpr/all_gather | solution.py:56
  223.3 5.7 %multiply_reduce_fusion.4 = (f32[32]{0:T(128)S(1)}, bf16[32,512]{1,0:T(8,128)(2,1)}, f32[32,512]{1,0:T(8,128)S(1)}) fusion(f32[512]{0:T(512)S(1)} %get-tuple-element.704, bf16[32,512]{1,0:T(8,128)(2,1)S(1)} %bitcast_select_fusion.5, f32[]{:T(128)} %get-tuple-element.702, bf16[32,8192]{1,0:T(8,128)(2,1)S(1)} %all_gather.9, ...), kind=kOutput, calls=%fused_computation.5.clone.1 | convolution fusion | flops 268615648 | bytes 9046148 | tf_op jit(solution)/shard_map/while/body/eval_jaxpr/dot_general | solution.py:57
  228.9 4.8 collective-permute-start
  235.8 18.7 %all_gather.9 = bf16[32,8192]{1,0:T(8,128)(2,1)S(1)} all-gather(bf16[32,512]{1,0:T(8,128)(2,1)S(1)} %bitcast_select_fusion.5), channel_id=1, replica_groups=mesh['section'=2,'mp'=16] {'mp'}, dimensions={1}, use_global_device_ids=true | all-gather | bytes 557056 | tf_op jit(solution)/shard_map/while/body/eval_jaxpr/all_gather | solution.py:56
  254.5 5.7 %multiply_reduce_fusion.4 = (f32[32]{0:T(128)S(1)}, bf16[32,512]{1,0:T(8,128)(2,1)}, f32[32,512]{1,0:T(8,128)S(1)}) fusion(f32[512]{0:T(512)S(1)} %get-tuple-element.704, bf16[32,512]{1,0:T(8,128)(2,1)S(1)} %bitcast_select_fusion.5, f32[]{:T(128)} %get-tuple-element.702, bf16[32,8192]{1,0:T(8,128)(2,1)S(1)} %all_gather.9, ...), kind=kOutput, calls=%fused_computation.5.clone.1 | convolution fusion | flops 268615648 | bytes 9046148 | tf_op jit(solution)/shard_map/while/body/eval_jaxpr/dot_general | solution.py:57
  260.1 4.8 collective-permute-start
  266.2 30.4 %psum.30 = f32[4,32]{1,0:T(4,128)S(1)} all-reduce(f32[4,32]{1,0:T(4,128)S(1)} %get-tuple-element.461), channel_id=1, replica_groups=mesh['section'=2,'mp'=16] {'mp'}, use_global_device_ids=true, to_apply=%region_7.8 | all-reduce | flops 128 | bytes 1024 | tf_op jit(solution)/shard_map/psum | solution.py:82
  297.4 155.4 %while.38 = (s32[]{:T(128)}, bf16[32,512]{1,0:T(8,128)(2,1)S(1)}, bf16[4,32,512]{2,1,0:T(8,128)(2,1)S(1)}, pred[]{:T(512)}, s32[]{:T(128)}, /*index=5*/f32[4,32]...) while((s32[]{:T(128)}, bf16[32,512]{1,0:T(8,128)(2,1)S(1)}, ...), condition=%wide.region_10.11_spmd, body=%wide.region_8.10_spmd.sunk | while | flops 269762784 | bytes 12787494 | solution.py:112
  297.4 5.9 %convolution_convert_fusion.2 = bf16[32,8192]{1,0:T(8,128)(2,1)S(1)} fusion(bf16[8192,512]{1,0:T(8,128)(2,1)} %get-tuple-element.748, f32[4,32,512]{2,1,0:T(8,128)S(1)} %get-tuple-element.747, s32[]{:T(128)S(6)} %min.21, bf16[32,512]{1,0:T(8,128)(2,1)S(1)} %get-tuple-element.725, f32[512]{0:T(512)S(1)} %get-tuple-element.746, f32[32]{0:T(128)S(1)} %fusion.37, ...), kind=kOutput, calls=%fused_computation.12.clone.1 | convolution fusion | flops 268910592 | bytes 9013765 | tf_op jit(solution)/shard_map/while/body/eval_jaxpr/dot_general | solution.py:96
  304.2 3.6 all-to-all-start
  307.8 14.2 %all-to-all-done = bf16[32,16,512]{2,0,1:T(8,128)(2,1)S(1)} async-done(((bf16[32,16,512]{2,0,1:T(8,128)(2,1)}), bf16[32,16,512]{2,0,1:T(8,128)(2,1)S(1)}, u32[]{:S(2)}, u32[]{:S(2)}) %all-to-all-start) | async-done | bytes 524320 | tf_op jit(solution)/shard_map/while/body/eval_jaxpr/all_to_all | solution.py:99
  322.2 1.3 collective-permute-start.1
  323.6 4.4 collective-permute-done.1
  328.0 5.9 %convolution_convert_fusion.2 = bf16[32,8192]{1,0:T(8,128)(2,1)S(1)} fusion(bf16[8192,512]{1,0:T(8,128)(2,1)} %get-tuple-element.748, f32[4,32,512]{2,1,0:T(8,128)S(1)} %get-tuple-element.747, s32[]{:T(128)S(6)} %min.21, bf16[32,512]{1,0:T(8,128)(2,1)S(1)} %get-tuple-element.725, f32[512]{0:T(512)S(1)} %get-tuple-element.746, f32[32]{0:T(128)S(1)} %fusion.37, ...), kind=kOutput, calls=%fused_computation.12.clone.1 | convolution fusion | flops 268910592 | bytes 9013765 | tf_op jit(solution)/shard_map/while/body/eval_jaxpr/dot_general | solution.py:96
  334.8 4.1 all-to-all-start
  338.9 14.2 %all-to-all-done = bf16[32,16,512]{2,0,1:T(8,128)(2,1)S(1)} async-done(((bf16[32,16,512]{2,0,1:T(8,128)(2,1)}), bf16[32,16,512]{2,0,1:T(8,128)(2,1)S(1)}, u32[]{:S(2)}, u32[]{:S(2)}) %all-to-all-start) | async-done | bytes 524320 | tf_op jit(solution)/shard_map/while/body/eval_jaxpr/all_to_all | solution.py:99
  353.3 1.3 collective-permute-start.1
  354.7 4.4 collective-permute-done.1
  359.1 5.9 %convolution_convert_fusion.2 = bf16[32,8192]{1,0:T(8,128)(2,1)S(1)} fusion(bf16[8192,512]{1,0:T(8,128)(2,1)} %get-tuple-element.748, f32[4,32,512]{2,1,0:T(8,128)S(1)} %get-tuple-element.747, s32[]{:T(128)S(6)} %min.21, bf16[32,512]{1,0:T(8,128)(2,1)S(1)} %get-tuple-element.725, f32[512]{0:T(512)S(1)} %get-tuple-element.746, f32[32]{0:T(128)S(1)} %fusion.37, ...), kind=kOutput, calls=%fused_computation.12.clone.1 | convolution fusion | flops 268910592 | bytes 9013765 | tf_op jit(solution)/shard_map/while/body/eval_jaxpr/dot_general | solution.py:96
  365.9 4.2 all-to-all-start
  370.1 14.2 %all-to-all-done = bf16[32,16,512]{2,0,1:T(8,128)(2,1)S(1)} async-done(((bf16[32,16,512]{2,0,1:T(8,128)(2,1)}), bf16[32,16,512]{2,0,1:T(8,128)(2,1)S(1)}, u32[]{:S(2)}, u32[]{:S(2)}) %all-to-all-start) | async-done | bytes 524320 | tf_op jit(solution)/shard_map/while/body/eval_jaxpr/all_to_all | solution.py:99
  384.5 1.3 collective-permute-start.1
  385.9 4.4 collective-permute-done.1
  390.4 5.9 %convolution_convert_fusion.2 = bf16[32,8192]{1,0:T(8,128)(2,1)S(1)} fusion(bf16[8192,512]{1,0:T(8,128)(2,1)} %get-tuple-element.748, f32[4,32,512]{2,1,0:T(8,128)S(1)} %get-tuple-element.747, s32[]{:T(128)S(6)} %min.21, bf16[32,512]{1,0:T(8,128)(2,1)S(1)} %get-tuple-element.725, f32[512]{0:T(512)S(1)} %get-tuple-element.746, f32[32]{0:T(128)S(1)} %fusion.37, ...), kind=kOutput, calls=%fused_computation.12.clone.1 | convolution fusion | flops 268910592 | bytes 9013765 | tf_op jit(solution)/shard_map/while/body/eval_jaxpr/dot_general | solution.py:96
  397.2 4.2 all-to-all-start
  401.3 14.2 %all-to-all-done = bf16[32,16,512]{2,0,1:T(8,128)(2,1)S(1)} async-done(((bf16[32,16,512]{2,0,1:T(8,128)(2,1)}), bf16[32,16,512]{2,0,1:T(8,128)(2,1)S(1)}, u32[]{:S(2)}, u32[]{:S(2)}) %all-to-all-start) | async-done | bytes 524320 | tf_op jit(solution)/shard_map/while/body/eval_jaxpr/all_to_all | solution.py:99
  415.8 1.3 collective-permute-start.1
  417.2 4.4 collective-permute-done.1
  421.6 5.9 %convolution_convert_fusion.2 = bf16[32,8192]{1,0:T(8,128)(2,1)S(1)} fusion(bf16[8192,512]{1,0:T(8,128)(2,1)} %get-tuple-element.748, f32[4,32,512]{2,1,0:T(8,128)S(1)} %get-tuple-element.747, s32[]{:T(128)S(6)} %min.21, bf16[32,512]{1,0:T(8,128)(2,1)S(1)} %get-tuple-element.725, f32[512]{0:T(512)S(1)} %get-tuple-element.746, f32[32]{0:T(128)S(1)} %fusion.37, ...), kind=kOutput, calls=%fused_computation.12.clone.1 | convolution fusion | flops 268910592 | bytes 9013765 | tf_op jit(solution)/shard_map/while/body/eval_jaxpr/dot_general | solution.py:96
  428.4 4.2 all-to-all-start
  432.6 14.2 %all-to-all-done = bf16[32,16,512]{2,0,1:T(8,128)(2,1)S(1)} async-done(((bf16[32,16,512]{2,0,1:T(8,128)(2,1)}), bf16[32,16,512]{2,0,1:T(8,128)(2,1)S(1)}, u32[]{:S(2)}, u32[]{:S(2)}) %all-to-all-start) | async-done | bytes 524320 | tf_op jit(solution)/shard_map/while/body/eval_jaxpr/all_to_all | solution.py:99
  448.4 4.4 collective-permute-done.1
  452.8 8.5 %fusion.13 = (f32[]{:T(128)}, bf16[1,8192,512]{2,1,0:T(8,128)(2,1)}) fusion(bf16[1,8192,512]{2,1,0:T(8,128)(2,1)} %bitcast.111, f32[]{:T(128)} %sqrt.3, bf16[4,32,8192]{2,1,0:T(8,128)(2,1)S(1)} %get-tuple-element.460, bf16[4,32,512]{2,1,0:T(8,128)(2,1)S(1)} %get-tuple-element.463), kind=kOutput, calls=%fused_computation.40 | convolution fusion | flops 1094713344 | bytes 19005448 | tf_op jit(solution)/shard_map/dot_general | solution.py:115
  461.3 31.7 %psum.31 = f32[]{:T(128)} all-reduce(f32[]{:T(128)} %get-tuple-element.513), channel_id=1, replica_groups=mesh['section'=2,'mp'=16] {'mp'}, use_global_device_ids=true, to_apply=%region_12.13 | all-reduce | flops 1 | bytes 8 | tf_op jit(solution)/shard_map/psum | solution.py:119
  (90 shorter events, 20.5 us)
Async XLA Ops:
  70.6 36.8 %copy-start = (f32[512]{0:T(512)S(1)}, f32[512]{0:T(512)}, u32[]{:S(2)}) copy-start(f32[512]{0:T(512)} %param.13) | copy-start | bytes 6148
  132.5 5.3 %collective-permute-start = (bf16[32,512]{1,0:T(8,128)(2,1)}, bf16[32,512]{1,0:T(8,128)(2,1)}, u32[]{:S(2)}, u32[]{:S(2)}) collective-permute-start(bf16[32,512]{1,0:T(8,128)(2,1)} %get-tuple-element.647), channel_id=1, source_target_pairs={{0,16},{1,17},{2,18},{3,19},{4,20},{5,21},{6,22},{7,23},{8,24},{9,... | collective-permute-start | bytes 98312 | tf_op jit(solution)/shard_map/while/body/eval_jaxpr/ppermute | solution.py:13
  164.7 6.1 %collective-permute-start = (bf16[32,512]{1,0:T(8,128)(2,1)}, bf16[32,512]{1,0:T(8,128)(2,1)}, u32[]{:S(2)}, u32[]{:S(2)}) collective-permute-start(bf16[32,512]{1,0:T(8,128)(2,1)} %get-tuple-element.647), channel_id=1, source_target_pairs={{0,16},{1,17},{2,18},{3,19},{4,20},{5,21},{6,22},{7,23},{8,24},{9,... | collective-permute-start | bytes 98312 | tf_op jit(solution)/shard_map/while/body/eval_jaxpr/ppermute | solution.py:13
  195.9 6.1 %collective-permute-start = (bf16[32,512]{1,0:T(8,128)(2,1)}, bf16[32,512]{1,0:T(8,128)(2,1)}, u32[]{:S(2)}, u32[]{:S(2)}) collective-permute-start(bf16[32,512]{1,0:T(8,128)(2,1)} %get-tuple-element.647), channel_id=1, source_target_pairs={{0,16},{1,17},{2,18},{3,19},{4,20},{5,21},{6,22},{7,23},{8,24},{9,... | collective-permute-start | bytes 98312 | tf_op jit(solution)/shard_map/while/body/eval_jaxpr/ppermute | solution.py:13
  228.9 6.1 %collective-permute-start = (bf16[32,512]{1,0:T(8,128)(2,1)}, bf16[32,512]{1,0:T(8,128)(2,1)}, u32[]{:S(2)}, u32[]{:S(2)}) collective-permute-start(bf16[32,512]{1,0:T(8,128)(2,1)} %get-tuple-element.647), channel_id=1, source_target_pairs={{0,16},{1,17},{2,18},{3,19},{4,20},{5,21},{6,22},{7,23},{8,24},{9,... | collective-permute-start | bytes 98312 | tf_op jit(solution)/shard_map/while/body/eval_jaxpr/ppermute | solution.py:13
  260.1 6.1 %collective-permute-start = (bf16[32,512]{1,0:T(8,128)(2,1)}, bf16[32,512]{1,0:T(8,128)(2,1)}, u32[]{:S(2)}, u32[]{:S(2)}) collective-permute-start(bf16[32,512]{1,0:T(8,128)(2,1)} %get-tuple-element.647), channel_id=1, source_target_pairs={{0,16},{1,17},{2,18},{3,19},{4,20},{5,21},{6,22},{7,23},{8,24},{9,... | collective-permute-start | bytes 98312 | tf_op jit(solution)/shard_map/while/body/eval_jaxpr/ppermute | solution.py:13
  304.2 17.8 %all-to-all-start = ((bf16[32,16,512]{2,0,1:T(8,128)(2,1)}), bf16[32,16,512]{2,0,1:T(8,128)(2,1)S(1)}, u32[]{:S(2)}, u32[]{:S(2)}) async-start(bf16[32,16,512]{2,0,1:T(8,128)(2,1)} %bitcast.109), calls=%async_computation | async-start | bytes 1048576 | tf_op jit(solution)/shard_map/while/body/eval_jaxpr/all_to_all | solution.py:99
  322.2 5.8 %collective-permute-start.1 = (bf16[32,512]{1,0:T(8,128)(2,1)S(1)}, bf16[32,512]{1,0:T(8,128)(2,1)S(1)}, u32[]{:S(2)}, u32[]{:S(2)}) collective-permute-start(bf16[32,512]{1,0:T(8,128)(2,1)S(1)} %fusion.38), channel_id=1, source_target_pairs={{16,0},{17,1},{18,2},{19,3},{20,4},{21,5},{22,6},{23,7},{24,8},{25... | collective-permute-start | bytes 98312 | tf_op jit(solution)/shard_map/while/body/eval_jaxpr/ppermute | solution.py:13
  334.8 18.4 %all-to-all-start = ((bf16[32,16,512]{2,0,1:T(8,128)(2,1)}), bf16[32,16,512]{2,0,1:T(8,128)(2,1)S(1)}, u32[]{:S(2)}, u32[]{:S(2)}) async-start(bf16[32,16,512]{2,0,1:T(8,128)(2,1)} %bitcast.109), calls=%async_computation | async-start | bytes 1048576 | tf_op jit(solution)/shard_map/while/body/eval_jaxpr/all_to_all | solution.py:99
  353.3 5.8 %collective-permute-start.1 = (bf16[32,512]{1,0:T(8,128)(2,1)S(1)}, bf16[32,512]{1,0:T(8,128)(2,1)S(1)}, u32[]{:S(2)}, u32[]{:S(2)}) collective-permute-start(bf16[32,512]{1,0:T(8,128)(2,1)S(1)} %fusion.38), channel_id=1, source_target_pairs={{16,0},{17,1},{18,2},{19,3},{20,4},{21,5},{22,6},{23,7},{24,8},{25... | collective-permute-start | bytes 98312 | tf_op jit(solution)/shard_map/while/body/eval_jaxpr/ppermute | solution.py:13
  365.9 18.4 %all-to-all-start = ((bf16[32,16,512]{2,0,1:T(8,128)(2,1)}), bf16[32,16,512]{2,0,1:T(8,128)(2,1)S(1)}, u32[]{:S(2)}, u32[]{:S(2)}) async-start(bf16[32,16,512]{2,0,1:T(8,128)(2,1)} %bitcast.109), calls=%async_computation | async-start | bytes 1048576 | tf_op jit(solution)/shard_map/while/body/eval_jaxpr/all_to_all | solution.py:99
  384.5 5.8 %collective-permute-start.1 = (bf16[32,512]{1,0:T(8,128)(2,1)S(1)}, bf16[32,512]{1,0:T(8,128)(2,1)S(1)}, u32[]{:S(2)}, u32[]{:S(2)}) collective-permute-start(bf16[32,512]{1,0:T(8,128)(2,1)S(1)} %fusion.38), channel_id=1, source_target_pairs={{16,0},{17,1},{18,2},{19,3},{20,4},{21,5},{22,6},{23,7},{24,8},{25... | collective-permute-start | bytes 98312 | tf_op jit(solution)/shard_map/while/body/eval_jaxpr/ppermute | solution.py:13
  397.2 18.4 %all-to-all-start = ((bf16[32,16,512]{2,0,1:T(8,128)(2,1)}), bf16[32,16,512]{2,0,1:T(8,128)(2,1)S(1)}, u32[]{:S(2)}, u32[]{:S(2)}) async-start(bf16[32,16,512]{2,0,1:T(8,128)(2,1)} %bitcast.109), calls=%async_computation | async-start | bytes 1048576 | tf_op jit(solution)/shard_map/while/body/eval_jaxpr/all_to_all | solution.py:99
  415.8 5.8 %collective-permute-start.1 = (bf16[32,512]{1,0:T(8,128)(2,1)S(1)}, bf16[32,512]{1,0:T(8,128)(2,1)S(1)}, u32[]{:S(2)}, u32[]{:S(2)}) collective-permute-start(bf16[32,512]{1,0:T(8,128)(2,1)S(1)} %fusion.38), channel_id=1, source_target_pairs={{16,0},{17,1},{18,2},{19,3},{20,4},{21,5},{22,6},{23,7},{24,8},{25... | collective-permute-start | bytes 98312 | tf_op jit(solution)/shard_map/while/body/eval_jaxpr/ppermute | solution.py:13
  428.4 18.4 %all-to-all-start = ((bf16[32,16,512]{2,0,1:T(8,128)(2,1)}), bf16[32,16,512]{2,0,1:T(8,128)(2,1)S(1)}, u32[]{:S(2)}, u32[]{:S(2)}) async-start(bf16[32,16,512]{2,0,1:T(8,128)(2,1)} %bitcast.109), calls=%async_computation | async-start | bytes 1048576 | tf_op jit(solution)/shard_map/while/body/eval_jaxpr/all_to_all | solution.py:99
  447.0 5.8 %collective-permute-start.1 = (bf16[32,512]{1,0:T(8,128)(2,1)S(1)}, bf16[32,512]{1,0:T(8,128)(2,1)S(1)}, u32[]{:S(2)}, u32[]{:S(2)}) collective-permute-start(bf16[32,512]{1,0:T(8,128)(2,1)S(1)} %fusion.38), channel_id=1, source_target_pairs={{16,0},{17,1},{18,2},{19,3},{20,4},{21,5},{22,6},{23,7},{24,8},{25... | collective-permute-start | bytes 98312 | tf_op jit(solution)/shard_map/while/body/eval_jaxpr/ppermute | solution.py:13
where the time goes:
time: 497 us; the launch traced here: 495 us
  blocking collectives  252 us (51%)
  waiting for transfers between devices  98.3 us (20%)
  matrix products  76.6 us (15%)
  starting transfers between devices  49.8 us (10%)
  other arithmetic  8.44 us (2%)
  local copies, waits for them, and re-layouts  5.69 us (1%)
    all_gather x5, blocking collectives, forward_tick(): shard_piece = lax.all_gather(layer_in, 'mp', axis=1, tiled=True)  97 us
    all_to_all x5, waiting for transfers between devices, backward_tick(): lax.all_to_all(partial_term.astype(jnp.bfloat16), 'mp', split_axis=1, con...  71.2 us
    psum x1, blocking collectives, power_step(): lax.psum(jnp.dot(weight, vector_bf, preferred_element_type=jnp.float32),...  63 us
    psum x1, blocking collectives, on_device(): lax.psum(jnp.sum(outer_sum * weight.astype(jnp.float32)), 'mp')  31.7 us
    psum x1, blocking collectives, on_device(): logits_all = lax.psum(partial_logits, 'mp')  30.4 us
    psum x1, blocking collectives, power_step(): norm_total = lax.psum(jnp.sum(right_part * right_part), 'mp')  30.1 us
    ppermute x10, starting transfers between devices, shifted(): return lax.ppermute(block, axis, route)  29.6 us
    dot_general x5, matrix products, backward_tick(): lax.dot_general(grad_pre, weight, (((1,), (1,)), ((), ())), preferred_ele...  29.6 us
  transfers between devices with their start and end apart: 15, of which 15 were waited for; matrix products, arithmetic and copies ran while one was open for 0% of the time, Pallas kernels for 0%

commit v1 on v0

--- a/solution.py
+++ b/solution.py
@@ -5,6 +5,17 @@
 
 loss_scale = 32.0
 tiny_eps = 1e-06
+
+
+def update_files(mine, axis_name):
+    x_now = mine
+    count_all = lax.axis_size(axis_name)
+    for tick in [j for j in (1, 2, 4, 8, 16) if j < count_all]:
+        upper = lax.ppermute(
+            x_now, axis_name=axis_name, perm=[(dd, dd ^ tick) for dd in range(count_all)]
+        )
+        x_now = x_now + upper
+    return x_now
 
 
 def shifted(block, axis, distance):
@@ -79,7 +90,7 @@
     _, inputs_all, pre_all, partial_logits, spectral, new_u = lax.fori_loop(
         0, tick_count, forward_tick, start_state
     )
-    logits_all = lax.psum(partial_logits, "mp")
+    logits_all = update_files(partial_logits, "mp")
 
     def backward_tick(tick_now, state_all):
         incoming, grad_all = state_all

time: 497 us -> 478 us (0.962)
  blocking collectives: 252 us -> 222 us
  waiting for transfers between devices: 98.3 us -> 108 us
    psum x1 -> x0, blocking collectives: 30.4 us -> none  [on_device(): logits_all = lax.psum(partial_logits, 'mp')]
    ppermute x0 -> x4, waiting for transfers between devices: none -> 9.68 us  [update_files(): lax.ppermute(x_now, axis_name=axis_name, perm=[(dd, dd ^ tick) for dd in...]
  transfers between devices with their start and end apart: 15 -> 19, of which waited for: 15 -> 19; matrix products, arithmetic and copies ran while one was open for 0% -> 1% of each run, Pallas kernels for 0% -> 0%
where the time goes in v1:
time: 478 us; the launch traced here: 476 us
  blocking collectives  222 us (46%)
  waiting for transfers between devices  108 us (23%)
  matrix products  76.6 us (16%)
  starting transfers between devices  51.6 us (11%)
  other arithmetic  8.44 us (2%)
  local copies, waits for them, and re-layouts  5.69 us (1%)
    all_gather x5, blocking collectives, forward_tick(): shard_piece = lax.all_gather(layer_in, 'mp', axis=1, tiled=True)  97 us
    all_to_all x5, waiting for transfers between devices, backward_tick(): lax.all_to_all(partial_term.astype(jnp.bfloat16), 'mp', split_axis=1, con...  71.2 us
    psum x1, blocking collectives, power_step(): lax.psum(jnp.dot(weight, vector_bf, preferred_element_type=jnp.float32),...  63 us
    psum x1, blocking collectives, on_device(): lax.psum(jnp.sum(outer_sum * weight.astype(jnp.float32)), 'mp')  31.7 us
    psum x1, blocking collectives, power_step(): norm_total = lax.psum(jnp.sum(right_part * right_part), 'mp')  30.1 us
    ppermute x10, starting transfers between devices, shifted(): return lax.ppermute(block, axis, route)  29.6 us
    dot_general x5, matrix products, backward_tick(): lax.dot_general(grad_pre, weight, (((1,), (1,)), ((), ())), preferred_ele...  29.6 us
    dot_general x5, matrix products, forward_tick(): jnp.dot(shard_piece, weight, preferred_element_type=jnp.float32)  28.3 us
  transfers between devices with their start and end apart: 19, of which 19 were waited for; matrix products, arithmetic and copies ran while one was open for 1% of the time, Pallas kernels for 0%

profile of v1, /device:TPU:0, one launch (start us, length us, event | category | flops | bytes accessed | tf_op | source)
XLA Modules:
  0.0 476.5 jit_solution(14155756928762305465)
XLA Ops:
  0.6 5.6 %fusion.15 = f32[1,8192]{1,0:T(1,128)S(1)} fusion(f32[1,512]{1,0:T(1,128)} %param.12, bf16[1,8192,512]{2,1,0:T(8,128)(2,1)} %param.11), kind=kOutput, calls=%fused_computation.44 | convolution fusion | flops 8389120 | bytes 8423424 | tf_op jit(solution)/shard_map/dot_general | solution.py:41
  6.3 63.0 %psum.21 = f32[8192]{0:T(1024)S(1)} all-reduce(f32[8192]{0:T(1024)S(1)} %bitcast.113), channel_id=1, replica_groups=mesh['section'=2,'mp'=16] {'mp'}, use_global_device_ids=true, to_apply=%region_0.0 | all-reduce | flops 8192 | bytes 65536 | tf_op jit(solution)/shard_map/psum | solution.py:41
  70.6 4.6 fusion.18
  75.8 30.1 %psum.22 = f32[]{:T(128)} all-reduce(f32[]{:T(128)} %multiply_reduce_fusion.2), channel_id=1, replica_groups=mesh['section'=2,'mp'=16] {'mp'}, use_global_device_ids=true, to_apply=%region_3.0 | all-reduce | flops 1 | bytes 8 | tf_op jit(solution)/shard_map/psum | solution.py:44
  107.4 158.8 %while.37 = (s32[]{:T(128)}, bf16[32,512]{1,0:T(8,128)(2,1)}, bf16[4,32,8192]{2,1,0:T(8,128)(2,1)S(1)}, f32[4,32,512]{2,1,0:T(8,128)S(1)}, f32[4,32]{1,0:T(4,128...) while((s32[]{:T(128)}, bf16[32,512]{1,0:T(8,128)(2,1)}, ...), condition=%wide.region_6.7_spmd, body=%wide.region_4.6_spmd.sunk | while | flops 268910592 | bytes 12782621 | solution.py:90
  108.2 18.7 %all_gather.9 = bf16[32,8192]{1,0:T(8,128)(2,1)S(1)} all-gather(bf16[32,512]{1,0:T(8,128)(2,1)S(1)} %bitcast_select_fusion.5), channel_id=1, replica_groups=mesh['section'=2,'mp'=16] {'mp'}, dimensions={1}, use_global_device_ids=true | all-gather | bytes 557056 | tf_op jit(solution)/shard_map/while/body/eval_jaxpr/all_gather | solution.py:67
  126.9 5.7 %multiply_reduce_fusion.4 = (f32[32]{0:T(128)S(1)}, bf16[32,512]{1,0:T(8,128)(2,1)}, f32[32,512]{1,0:T(8,128)S(1)}) fusion(f32[512]{0:T(512)S(1)} %get-tuple-element.704, bf16[32,512]{1,0:T(8,128)(2,1)S(1)} %bitcast_select_fusion.5, f32[]{:T(128)} %get-tuple-element.702, bf16[32,8192]{1,0:T(8,128)(2,1)S(1)} %all_gather.9, ...), kind=kOutput, calls=%fused_computation.5.clone.1 | convolution fusion | flops 268615648 | bytes 9046148 | tf_op jit(solution)/shard_map/while/body/eval_jaxpr/dot_general | solution.py:68
  132.5 4.0 collective-permute-start
  138.6 20.4 %all_gather.9 = bf16[32,8192]{1,0:T(8,128)(2,1)S(1)} all-gather(bf16[32,512]{1,0:T(8,128)(2,1)S(1)} %bitcast_select_fusion.5), channel_id=1, replica_groups=mesh['section'=2,'mp'=16] {'mp'}, dimensions={1}, use_global_device_ids=true | all-gather | bytes 557056 | tf_op jit(solution)/shard_map/while/body/eval_jaxpr/all_gather | solution.py:67
  159.1 5.7 %multiply_reduce_fusion.4 = (f32[32]{0:T(128)S(1)}, bf16[32,512]{1,0:T(8,128)(2,1)}, f32[32,512]{1,0:T(8,128)S(1)}) fusion(f32[512]{0:T(512)S(1)} %get-tuple-element.704, bf16[32,512]{1,0:T(8,128)(2,1)S(1)} %bitcast_select_fusion.5, f32[]{:T(128)} %get-tuple-element.702, bf16[32,8192]{1,0:T(8,128)(2,1)S(1)} %all_gather.9, ...), kind=kOutput, calls=%fused_computation.5.clone.1 | convolution fusion | flops 268615648 | bytes 9046148 | tf_op jit(solution)/shard_map/while/body/eval_jaxpr/dot_general | solution.py:68
  164.7 4.8 collective-permute-start
  171.6 18.7 %all_gather.9 = bf16[32,8192]{1,0:T(8,128)(2,1)S(1)} all-gather(bf16[32,512]{1,0:T(8,128)(2,1)S(1)} %bitcast_select_fusion.5), channel_id=1, replica_groups=mesh['section'=2,'mp'=16] {'mp'}, dimensions={1}, use_global_device_ids=true | all-gather | bytes 557056 | tf_op jit(solution)/shard_map/while/body/eval_jaxpr/all_gather | solution.py:67
  190.3 5.7 %multiply_reduce_fusion.4 = (f32[32]{0:T(128)S(1)}, bf16[32,512]{1,0:T(8,128)(2,1)}, f32[32,512]{1,0:T(8,128)S(1)}) fusion(f32[512]{0:T(512)S(1)} %get-tuple-element.704, bf16[32,512]{1,0:T(8,128)(2,1)S(1)} %bitcast_select_fusion.5, f32[]{:T(128)} %get-tuple-element.702, bf16[32,8192]{1,0:T(8,128)(2,1)S(1)} %all_gather.9, ...), kind=kOutput, calls=%fused_computation.5.clone.1 | convolution fusion | flops 268615648 | bytes 9046148 | tf_op jit(solution)/shard_map/while/body/eval_jaxpr/dot_general | solution.py:68
  195.9 4.8 %collective-permute-start = (bf16[32,512]{1,0:T(8,128)(2,1)}, bf16[32,512]{1,0:T(8,128)(2,1)}, u32[]{:S(2)}, u32[]{:S(2)}) collective-permute-start(bf16[32,512]{1,0:T(8,128)(2,1)} %get-tuple-element.647), channel_id=1, source_target_pairs={{0,16},{1,17},{2,18},{3,19},{4,20},{5,21},{6,22},{7,23},{8,24},{9,... | collective-permute-start | bytes 98312 | tf_op jit(solution)/shard_map/while/body/eval_jaxpr/ppermute | solution.py:24
  202.8 20.4 %all_gather.9 = bf16[32,8192]{1,0:T(8,128)(2,1)S(1)} all-gather(bf16[32,512]{1,0:T(8,128)(2,1)S(1)} %bitcast_select_fusion.5), channel_id=1, replica_groups=mesh['section'=2,'mp'=16] {'mp'}, dimensions={1}, use_global_device_ids=true | all-gather | bytes 557056 | tf_op jit(solution)/shard_map/while/body/eval_jaxpr/all_gather | solution.py:67
  223.3 5.7 %multiply_reduce_fusion.4 = (f32[32]{0:T(128)S(1)}, bf16[32,512]{1,0:T(8,128)(2,1)}, f32[32,512]{1,0:T(8,128)S(1)}) fusion(f32[512]{0:T(512)S(1)} %get-tuple-element.704, bf16[32,512]{1,0:T(8,128)(2,1)S(1)} %bitcast_select_fusion.5, f32[]{:T(128)} %get-tuple-element.702, bf16[32,8192]{1,0:T(8,128)(2,1)S(1)} %all_gather.9, ...), kind=kOutput, calls=%fused_computation.5.clone.1 | convolution fusion | flops 268615648 | bytes 9046148 | tf_op jit(solution)/shard_map/while/body/eval_jaxpr/dot_general | solution.py:68
  228.9 4.8 %collective-permute-start = (bf16[32,512]{1,0:T(8,128)(2,1)}, bf16[32,512]{1,0:T(8,128)(2,1)}, u32[]{:S(2)}, u32[]{:S(2)}) collective-permute-start(bf16[32,512]{1,0:T(8,128)(2,1)} %get-tuple-element.647), channel_id=1, source_target_pairs={{0,16},{1,17},{2,18},{3,19},{4,20},{5,21},{6,22},{7,23},{8,24},{9,... | collective-permute-start | bytes 98312 | tf_op jit(solution)/shard_map/while/body/eval_jaxpr/ppermute | solution.py:24
  235.8 18.7 %all_gather.9 = bf16[32,8192]{1,0:T(8,128)(2,1)S(1)} all-gather(bf16[32,512]{1,0:T(8,128)(2,1)S(1)} %bitcast_select_fusion.5), channel_id=1, replica_groups=mesh['section'=2,'mp'=16] {'mp'}, dimensions={1}, use_global_device_ids=true | all-gather | bytes 557056 | tf_op jit(solution)/shard_map/while/body/eval_jaxpr/all_gather | solution.py:67
  254.5 5.7 %multiply_reduce_fusion.4 = (f32[32]{0:T(128)S(1)}, bf16[32,512]{1,0:T(8,128)(2,1)}, f32[32,512]{1,0:T(8,128)S(1)}) fusion(f32[512]{0:T(512)S(1)} %get-tuple-element.704, bf16[32,512]{1,0:T(8,128)(2,1)S(1)} %bitcast_select_fusion.5, f32[]{:T(128)} %get-tuple-element.702, bf16[32,8192]{1,0:T(8,128)(2,1)S(1)} %all_gather.9, ...), kind=kOutput, calls=%fused_computation.5.clone.1 | convolution fusion | flops 268615648 | bytes 9046148 | tf_op jit(solution)/shard_map/while/body/eval_jaxpr/dot_general | solution.py:68
  260.1 4.8 %collective-permute-start = (bf16[32,512]{1,0:T(8,128)(2,1)}, bf16[32,512]{1,0:T(8,128)(2,1)}, u32[]{:S(2)}, u32[]{:S(2)}) collective-permute-start(bf16[32,512]{1,0:T(8,128)(2,1)} %get-tuple-element.647), channel_id=1, source_target_pairs={{0,16},{1,17},{2,18},{3,19},{4,20},{5,21},{6,22},{7,23},{8,24},{9,... | collective-permute-start | bytes 98312 | tf_op jit(solution)/shard_map/while/body/eval_jaxpr/ppermute | solution.py:24
  267.4 1.9 collective-permute-start.3
  269.3 1.7 collective-permute-done.3
  271.6 3.0 collective-permute-done.4
  275.3 3.8 collective-permute-done.5
  279.1 155.4 %while.38 = (s32[]{:T(128)}, bf16[32,512]{1,0:T(8,128)(2,1)S(1)}, bf16[4,32,512]{2,1,0:T(8,128)(2,1)S(1)}, pred[]{:T(512)}, s32[]{:T(128)}, /*index=5*/f32[4,32]...) while((s32[]{:T(128)}, bf16[32,512]{1,0:T(8,128)(2,1)S(1)}, ...), condition=%wide.region_9.10_spmd, body=%wide.region_7.9_spmd.sunk | while | flops 269762784 | bytes 12787494 | solution.py:123
  279.1 5.9 %convolution_convert_fusion.2 = bf16[32,8192]{1,0:T(8,128)(2,1)S(1)} fusion(bf16[8192,512]{1,0:T(8,128)(2,1)} %get-tuple-element.748, f32[4,32,512]{2,1,0:T(8,128)S(1)} %get-tuple-element.747, s32[]{:T(128)S(6)} %min.21, bf16[32,512]{1,0:T(8,128)(2,1)S(1)} %get-tuple-element.725, f32[512]{0:T(512)S(1)} %get-tuple-element.746, f32[32]{0:T(128)S(1)} %fusion.37, ...), kind=kOutput, calls=%fused_computation.12.clone.1 | convolution fusion | flops 268910592 | bytes 9013765 | tf_op jit(solution)/shard_map/while/body/eval_jaxpr/dot_general | solution.py:107
  285.9 3.6 all-to-all-start
  289.5 14.2 %all-to-all-done = bf16[32,16,512]{2,0,1:T(8,128)(2,1)S(1)} async-done(((bf16[32,16,512]{2,0,1:T(8,128)(2,1)}), bf16[32,16,512]{2,0,1:T(8,128)(2,1)S(1)}, u32[]{:S(2)}, u32[]{:S(2)}) %all-to-all-start) | async-done | bytes 524320 | tf_op jit(solution)/shard_map/while/body/eval_jaxpr/all_to_all | solution.py:110
  305.3 4.4 collective-permute-done.1
  309.7 5.9 %convolution_convert_fusion.2 = bf16[32,8192]{1,0:T(8,128)(2,1)S(1)} fusion(bf16[8192,512]{1,0:T(8,128)(2,1)} %get-tuple-element.748, f32[4,32,512]{2,1,0:T(8,128)S(1)} %get-tuple-element.747, s32[]{:T(128)S(6)} %min.21, bf16[32,512]{1,0:T(8,128)(2,1)S(1)} %get-tuple-element.725, f32[512]{0:T(512)S(1)} %get-tuple-element.746, f32[32]{0:T(128)S(1)} %fusion.37, ...), kind=kOutput, calls=%fused_computation.12.clone.1 | convolution fusion | flops 268910592 | bytes 9013765 | tf_op jit(solution)/shard_map/while/body/eval_jaxpr/dot_general | solution.py:107
  316.5 4.1 all-to-all-start
  320.6 14.2 %all-to-all-done = bf16[32,16,512]{2,0,1:T(8,128)(2,1)S(1)} async-done(((bf16[32,16,512]{2,0,1:T(8,128)(2,1)}), bf16[32,16,512]{2,0,1:T(8,128)(2,1)S(1)}, u32[]{:S(2)}, u32[]{:S(2)}) %all-to-all-start) | async-done | bytes 524320 | tf_op jit(solution)/shard_map/while/body/eval_jaxpr/all_to_all | solution.py:110
  335.0 1.3 collective-permute-start.1
  336.4 4.4 collective-permute-done.1
  340.9 5.9 %convolution_convert_fusion.2 = bf16[32,8192]{1,0:T(8,128)(2,1)S(1)} fusion(bf16[8192,512]{1,0:T(8,128)(2,1)} %get-tuple-element.748, f32[4,32,512]{2,1,0:T(8,128)S(1)} %get-tuple-element.747, s32[]{:T(128)S(6)} %min.21, bf16[32,512]{1,0:T(8,128)(2,1)S(1)} %get-tuple-element.725, f32[512]{0:T(512)S(1)} %get-tuple-element.746, f32[32]{0:T(128)S(1)} %fusion.37, ...), kind=kOutput, calls=%fused_computation.12.clone.1 | convolution fusion | flops 268910592 | bytes 9013765 | tf_op jit(solution)/shard_map/while/body/eval_jaxpr/dot_general | solution.py:107
  347.7 4.2 all-to-all-start
  351.9 14.2 %all-to-all-done = bf16[32,16,512]{2,0,1:T(8,128)(2,1)S(1)} async-done(((bf16[32,16,512]{2,0,1:T(8,128)(2,1)}), bf16[32,16,512]{2,0,1:T(8,128)(2,1)S(1)}, u32[]{:S(2)}, u32[]{:S(2)}) %all-to-all-start) | async-done | bytes 524320 | tf_op jit(solution)/shard_map/while/body/eval_jaxpr/all_to_all | solution.py:110
  367.7 4.4 collective-permute-done.1
  372.1 5.9 %convolution_convert_fusion.2 = bf16[32,8192]{1,0:T(8,128)(2,1)S(1)} fusion(bf16[8192,512]{1,0:T(8,128)(2,1)} %get-tuple-element.748, f32[4,32,512]{2,1,0:T(8,128)S(1)} %get-tuple-element.747, s32[]{:T(128)S(6)} %min.21, bf16[32,512]{1,0:T(8,128)(2,1)S(1)} %get-tuple-element.725, f32[512]{0:T(512)S(1)} %get-tuple-element.746, f32[32]{0:T(128)S(1)} %fusion.37, ...), kind=kOutput, calls=%fused_computation.12.clone.1 | convolution fusion | flops 268910592 | bytes 9013765 | tf_op jit(solution)/shard_map/while/body/eval_jaxpr/dot_general | solution.py:107
  378.9 4.2 all-to-all-start
  383.1 14.2 %all-to-all-done = bf16[32,16,512]{2,0,1:T(8,128)(2,1)S(1)} async-done(((bf16[32,16,512]{2,0,1:T(8,128)(2,1)}), bf16[32,16,512]{2,0,1:T(8,128)(2,1)S(1)}, u32[]{:S(2)}, u32[]{:S(2)}) %all-to-all-start) | async-done | bytes 524320 | tf_op jit(solution)/shard_map/while/body/eval_jaxpr/all_to_all | solution.py:110
  398.9 4.4 collective-permute-done.1
  403.3 5.9 %convolution_convert_fusion.2 = bf16[32,8192]{1,0:T(8,128)(2,1)S(1)} fusion(bf16[8192,512]{1,0:T(8,128)(2,1)} %get-tuple-element.748, f32[4,32,512]{2,1,0:T(8,128)S(1)} %get-tuple-element.747, s32[]{:T(128)S(6)} %min.21, bf16[32,512]{1,0:T(8,128)(2,1)S(1)} %get-tuple-element.725, f32[512]{0:T(512)S(1)} %get-tuple-element.746, f32[32]{0:T(128)S(1)} %fusion.37, ...), kind=kOutput, calls=%fused_computation.12.clone.1 | convolution fusion | flops 268910592 | bytes 9013765 | tf_op jit(solution)/shard_map/while/body/eval_jaxpr/dot_general | solution.py:107
  410.1 4.2 all-to-all-start
  414.3 14.2 %all-to-all-done = bf16[32,16,512]{2,0,1:T(8,128)(2,1)S(1)} async-done(((bf16[32,16,512]{2,0,1:T(8,128)(2,1)}), bf16[32,16,512]{2,0,1:T(8,128)(2,1)S(1)}, u32[]{:S(2)}, u32[]{:S(2)}) %all-to-all-start) | async-done | bytes 524320 | tf_op jit(solution)/shard_map/while/body/eval_jaxpr/all_to_all | solution.py:110
  430.1 4.4 collective-permute-done.1
  434.5 8.5 %fusion.13 = (f32[]{:T(128)}, bf16[1,8192,512]{2,1,0:T(8,128)(2,1)}) fusion(bf16[1,8192,512]{2,1,0:T(8,128)(2,1)} %bitcast.111, f32[]{:T(128)} %sqrt.3, bf16[4,32,8192]{2,1,0:T(8,128)(2,1)S(1)} %get-tuple-element.460, bf16[4,32,512]{2,1,0:T(8,128)(2,1)S(1)} %get-tuple-element.463), kind=kOutput, calls=%fused_computation.40 | convolution fusion | flops 1094713344 | bytes 19005448 | tf_op jit(solution)/shard_map/dot_general | solution.py:126
  443.0 31.7 %psum.23 = f32[]{:T(128)} all-reduce(f32[]{:T(128)} %get-tuple-element.513), channel_id=1, replica_groups=mesh['section'=2,'mp'=16] {'mp'}, use_global_device_ids=true, to_apply=%region_11.12 | all-reduce | flops 1 | bytes 8 | tf_op jit(solution)/shard_map/psum | solution.py:130
  (101 shorter events, 25.5 us)
Async XLA Ops:
  70.6 36.8 %copy-start = (f32[512]{0:T(512)S(1)}, f32[512]{0:T(512)}, u32[]{:S(2)}) copy-start(f32[512]{0:T(512)} %param.13) | copy-start | bytes 6148
  132.5 5.3 %collective-permute-start = (bf16[32,512]{1,0:T(8,128)(2,1)}, bf16[32,512]{1,0:T(8,128)(2,1)}, u32[]{:S(2)}, u32[]{:S(2)}) collective-permute-start(bf16[32,512]{1,0:T(8,128)(2,1)} %get-tuple-element.647), channel_id=1, source_target_pairs={{0,16},{1,17},{2,18},{3,19},{4,20},{5,21},{6,22},{7,23},{8,24},{9,... | collective-permute-start | bytes 98312 | tf_op jit(solution)/shard_map/while/body/eval_jaxpr/ppermute | solution.py:24
  164.7 6.1 %collective-permute-start = (bf16[32,512]{1,0:T(8,128)(2,1)}, bf16[32,512]{1,0:T(8,128)(2,1)}, u32[]{:S(2)}, u32[]{:S(2)}) collective-permute-start(bf16[32,512]{1,0:T(8,128)(2,1)} %get-tuple-element.647), channel_id=1, source_target_pairs={{0,16},{1,17},{2,18},{3,19},{4,20},{5,21},{6,22},{7,23},{8,24},{9,... | collective-permute-start | bytes 98312 | tf_op jit(solution)/shard_map/while/body/eval_jaxpr/ppermute | solution.py:24
  195.9 6.1 %collective-permute-start = (bf16[32,512]{1,0:T(8,128)(2,1)}, bf16[32,512]{1,0:T(8,128)(2,1)}, u32[]{:S(2)}, u32[]{:S(2)}) collective-permute-start(bf16[32,512]{1,0:T(8,128)(2,1)} %get-tuple-element.647), channel_id=1, source_target_pairs={{0,16},{1,17},{2,18},{3,19},{4,20},{5,21},{6,22},{7,23},{8,24},{9,... | collective-permute-start | bytes 98312 | tf_op jit(solution)/shard_map/while/body/eval_jaxpr/ppermute | solution.py:24
  228.9 6.1 %collective-permute-start = (bf16[32,512]{1,0:T(8,128)(2,1)}, bf16[32,512]{1,0:T(8,128)(2,1)}, u32[]{:S(2)}, u32[]{:S(2)}) collective-permute-start(bf16[32,512]{1,0:T(8,128)(2,1)} %get-tuple-element.647), channel_id=1, source_target_pairs={{0,16},{1,17},{2,18},{3,19},{4,20},{5,21},{6,22},{7,23},{8,24},{9,... | collective-permute-start | bytes 98312 | tf_op jit(solution)/shard_map/while/body/eval_jaxpr/ppermute | solution.py:24
  260.1 6.1 %collective-permute-start = (bf16[32,512]{1,0:T(8,128)(2,1)}, bf16[32,512]{1,0:T(8,128)(2,1)}, u32[]{:S(2)}, u32[]{:S(2)}) collective-permute-start(bf16[32,512]{1,0:T(8,128)(2,1)} %get-tuple-element.647), channel_id=1, source_target_pairs={{0,16},{1,17},{2,18},{3,19},{4,20},{5,21},{6,22},{7,23},{8,24},{9,... | collective-permute-start | bytes 98312 | tf_op jit(solution)/shard_map/while/body/eval_jaxpr/ppermute | solution.py:24
  266.2 1.2 collective-permute-start.2
  267.4 3.6 collective-permute-start.3
  271.0 3.6 collective-permute-start.4
  274.6 4.5 collective-permute-start.5
  285.9 17.8 %all-to-all-start = ((bf16[32,16,512]{2,0,1:T(8,128)(2,1)}), bf16[32,16,512]{2,0,1:T(8,128)(2,1)S(1)}, u32[]{:S(2)}, u32[]{:S(2)}) async-start(bf16[32,16,512]{2,0,1:T(8,128)(2,1)} %bitcast.109), calls=%async_computation | async-start | bytes 1048576 | tf_op jit(solution)/shard_map/while/body/eval_jaxpr/all_to_all | solution.py:110
  303.9 5.8 %collective-permute-start.1 = (bf16[32,512]{1,0:T(8,128)(2,1)S(1)}, bf16[32,512]{1,0:T(8,128)(2,1)S(1)}, u32[]{:S(2)}, u32[]{:S(2)}) collective-permute-start(bf16[32,512]{1,0:T(8,128)(2,1)S(1)} %fusion.38), channel_id=1, source_target_pairs={{16,0},{17,1},{18,2},{19,3},{20,4},{21,5},{22,6},{23,7},{24,8},{25... | collective-permute-start | bytes 98312 | tf_op jit(solution)/shard_map/while/body/eval_jaxpr/ppermute | solution.py:24
  316.5 18.4 %all-to-all-start = ((bf16[32,16,512]{2,0,1:T(8,128)(2,1)}), bf16[32,16,512]{2,0,1:T(8,128)(2,1)S(1)}, u32[]{:S(2)}, u32[]{:S(2)}) async-start(bf16[32,16,512]{2,0,1:T(8,128)(2,1)} %bitcast.109), calls=%async_computation | async-start | bytes 1048576 | tf_op jit(solution)/shard_map/while/body/eval_jaxpr/all_to_all | solution.py:110
  335.0 5.8 %collective-permute-start.1 = (bf16[32,512]{1,0:T(8,128)(2,1)S(1)}, bf16[32,512]{1,0:T(8,128)(2,1)S(1)}, u32[]{:S(2)}, u32[]{:S(2)}) collective-permute-start(bf16[32,512]{1,0:T(8,128)(2,1)S(1)} %fusion.38), channel_id=1, source_target_pairs={{16,0},{17,1},{18,2},{19,3},{20,4},{21,5},{22,6},{23,7},{24,8},{25... | collective-permute-start | bytes 98312 | tf_op jit(solution)/shard_map/while/body/eval_jaxpr/ppermute | solution.py:24
  347.7 18.4 %all-to-all-start = ((bf16[32,16,512]{2,0,1:T(8,128)(2,1)}), bf16[32,16,512]{2,0,1:T(8,128)(2,1)S(1)}, u32[]{:S(2)}, u32[]{:S(2)}) async-start(bf16[32,16,512]{2,0,1:T(8,128)(2,1)} %bitcast.109), calls=%async_computation | async-start | bytes 1048576 | tf_op jit(solution)/shard_map/while/body/eval_jaxpr/all_to_all | solution.py:110
  366.3 5.8 %collective-permute-start.1 = (bf16[32,512]{1,0:T(8,128)(2,1)S(1)}, bf16[32,512]{1,0:T(8,128)(2,1)S(1)}, u32[]{:S(2)}, u32[]{:S(2)}) collective-permute-start(bf16[32,512]{1,0:T(8,128)(2,1)S(1)} %fusion.38), channel_id=1, source_target_pairs={{16,0},{17,1},{18,2},{19,3},{20,4},{21,5},{22,6},{23,7},{24,8},{25... | collective-permute-start | bytes 98312 | tf_op jit(solution)/shard_map/while/body/eval_jaxpr/ppermute | solution.py:24
  378.9 18.4 %all-to-all-start = ((bf16[32,16,512]{2,0,1:T(8,128)(2,1)}), bf16[32,16,512]{2,0,1:T(8,128)(2,1)S(1)}, u32[]{:S(2)}, u32[]{:S(2)}) async-start(bf16[32,16,512]{2,0,1:T(8,128)(2,1)} %bitcast.109), calls=%async_computation | async-start | bytes 1048576 | tf_op jit(solution)/shard_map/while/body/eval_jaxpr/all_to_all | solution.py:110
  397.5 5.8 %collective-permute-start.1 = (bf16[32,512]{1,0:T(8,128)(2,1)S(1)}, bf16[32,512]{1,0:T(8,128)(2,1)S(1)}, u32[]{:S(2)}, u32[]{:S(2)}) collective-permute-start(bf16[32,512]{1,0:T(8,128)(2,1)S(1)} %fusion.38), channel_id=1, source_target_pairs={{16,0},{17,1},{18,2},{19,3},{20,4},{21,5},{22,6},{23,7},{24,8},{25... | collective-permute-start | bytes 98312 | tf_op jit(solution)/shard_map/while/body/eval_jaxpr/ppermute | solution.py:24
  410.1 18.4 %all-to-all-start = ((bf16[32,16,512]{2,0,1:T(8,128)(2,1)}), bf16[32,16,512]{2,0,1:T(8,128)(2,1)S(1)}, u32[]{:S(2)}, u32[]{:S(2)}) async-start(bf16[32,16,512]{2,0,1:T(8,128)(2,1)} %bitcast.109), calls=%async_computation | async-start | bytes 1048576 | tf_op jit(solution)/shard_map/while/body/eval_jaxpr/all_to_all | solution.py:110
  428.7 5.8 %collective-permute-start.1 = (bf16[32,512]{1,0:T(8,128)(2,1)S(1)}, bf16[32,512]{1,0:T(8,128)(2,1)S(1)}, u32[]{:S(2)}, u32[]{:S(2)}) collective-permute-start(bf16[32,512]{1,0:T(8,128)(2,1)S(1)} %fusion.38), channel_id=1, source_target_pairs={{16,0},{17,1},{18,2},{19,3},{20,4},{21,5},{22,6},{23,7},{24,8},{25... | collective-permute-start | bytes 98312 | tf_op jit(solution)/shard_map/while/body/eval_jaxpr/ppermute | solution.py:24
